TPU v7x, 32 devices: a whole 2x2x4 slice. The times are simulated.
32 devices in a mesh: seq: 4 (over z), tensor: 2 (over x), dp: 4 (over y, core).
Axes of the slice: x: 2, y: 2, z: 4, core: 2. Of those that a mesh axis runs over, the one named last changes fastest.
Arguments:
- tokens: bfloat16 [4, 1024, 3072], P('dp', 'seq'), may hold values from -6 to 6
- cotangent: bfloat16 [4, 1024, 3072], P('dp', 'seq'), may hold values from -6 to 6
- qkv_weight: bfloat16 [3072, 3, 768], P(('seq', 'dp'), None, 'tensor'), may hold values from -0.109375 to 0.109375
- out_weight: bfloat16 [3072, 768], P(('seq', 'dp'), 'tensor'), may hold values from -0.21875 to 0.21875
Outputs:
- qkv_grad: float32 [3072, 3, 768], P(('seq', 'dp'), None, 'tensor')
- out_grad: float32 [3072, 768], P(('seq', 'dp'), 'tensor')
- branch_grad: bfloat16 [4, 1024, 3072], P('dp', 'seq', 'tensor')
All inputs are finite; a program needn't handle non-finite values.
Results may differ from a plain program's by a relative error of at most 0.025.
Values may be sent and summed in bfloat16 or wider, within the bound.
A program may use at most 128 MiB of HBM per device.

v0:
```python
import jax
import jax.numpy as jnp
from jax import lax
from jax.sharding import PartitionSpec as P

HD = 128
epsilon = 1e-06


def normalize(values):
    average = jnp.mean(values, axis=-1, keepdims=True)
    centered = values - average
    inverse = lax.rsqrt(jnp.mean(centered * centered, axis=-1, keepdims=True) + epsilon)
    return (centered * inverse, inverse)


def normalize_back(gradient, normed, inverse):
    mean_grad = jnp.mean(gradient, axis=-1, keepdims=True)
    mean_both = jnp.mean(gradient * normed, axis=-1, keepdims=True)
    return (gradient - mean_grad - normed * mean_both) * inverse


def local(tokens, cotangent, qkv_weight, out_weight):
    row_count = tokens.shape[1]
    feature_count = tokens.shape[2]
    column_count = out_weight.shape[1]
    head_count = column_count // HD
    score_scale = HD ** (-0.5)
    own_rows = qkv_weight.shape[0]
    grad_rows = cotangent[0]
    normed, inverse = normalize(tokens[0].astype(jnp.float32))
    unit_low = normed.astype(jnp.bfloat16)
    flat_weight = qkv_weight.reshape(own_rows, 3 * column_count)
    piece_qkv = lax.all_gather(flat_weight, ("seq", "dp"), axis=0, tiled=True)
    piece_out = lax.all_gather(out_weight, ("seq", "dp"), axis=0, tiled=True)
    piece_rows = piece_qkv.shape[0]
    left_rows = unit_low
    right_rows = grad_rows
    projected = jnp.dot(left_rows, piece_qkv, preferred_element_type=jnp.float32)
    attended_grad = jnp.dot(right_rows, piece_out, preferred_element_type=jnp.float32)
    full_qkv = piece_qkv
    projected, attended_grad, full_qkv = (projected, attended_grad, full_qkv)
    query_unit, query_inv = normalize(
        projected[:, :column_count].reshape(row_count, head_count, HD)
    )
    key_unit, key_inv = normalize(
        projected[:, column_count : 2 * column_count].reshape(row_count, head_count, HD)
    )
    query_low = query_unit.astype(jnp.bfloat16)
    key_value = jnp.stack(
        [
            key_unit.astype(jnp.bfloat16).reshape(row_count, column_count),
            projected[:, 2 * column_count :].astype(jnp.bfloat16),
        ]
    )
    grad_low = attended_grad.astype(jnp.bfloat16).reshape(row_count, head_count, HD)

    def scores_of(key_rows):
        piece_rows = key_rows.shape[0]
        return (
            jnp.einsum(
                "qhd,khd->hqk",
                query_low,
                key_rows.reshape(piece_rows, head_count, HD),
                preferred_element_type=jnp.float32,
            )
            * score_scale
        )

    every_pair = lax.all_gather(key_value, "seq", axis=1, tiled=True)
    piece_rows = every_pair.shape[1]
    exponent = jnp.exp(scores_of(every_pair[0]))
    add_exp_total = jnp.sum(exponent, axis=-1)
    weighted = jnp.einsum(
        "hqk,khd->qhd",
        exponent.astype(jnp.bfloat16),
        every_pair[1].reshape(piece_rows, head_count, HD),
        preferred_element_type=jnp.float32,
    )
    exp_total, weighted = (add_exp_total, weighted)
    attended_low = (weighted / exp_total.T[:, :, None]).astype(jnp.bfloat16)
    row_delta = jnp.sum(grad_low.astype(jnp.float32) * attended_low.astype(jnp.float32), axis=-1)
    piece_rows = every_pair.shape[1]
    key_rows = every_pair[0].reshape(piece_rows, head_count, HD)
    value_rows = every_pair[1].reshape(piece_rows, head_count, HD)
    probability = jnp.exp(scores_of(every_pair[0])) / exp_total[:, :, None]
    prob_grad = jnp.einsum("qhd,khd->hqk", grad_low, value_rows, preferred_element_type=jnp.float32)
    grad_score = (probability * (prob_grad - row_delta.T[:, :, None]) * score_scale).astype(
        jnp.bfloat16
    )
    query_part = jnp.einsum(
        "hqk,khd->qhd", grad_score, key_rows, preferred_element_type=jnp.float32
    )
    key_part = jnp.einsum("hqk,qhd->khd", grad_score, query_low, preferred_element_type=jnp.float32)
    value_part = jnp.einsum(
        "hqk,qhd->khd",
        probability.astype(jnp.bfloat16),
        grad_low,
        preferred_element_type=jnp.float32,
    )
    every_grad = jnp.stack(
        [key_part.reshape(piece_rows, column_count), value_part.reshape(piece_rows, column_count)]
    )
    pair_grad = lax.psum_scatter(
        every_grad.astype(jnp.bfloat16), "seq", scatter_dimension=1, tiled=True
    ).astype(jnp.float32)
    query_back = normalize_back(query_part, query_unit, query_inv)
    key_back = normalize_back(pair_grad[0].reshape(row_count, head_count, HD), key_unit, key_inv)
    qkv_low = jnp.concatenate(
        [
            query_back.reshape(row_count, column_count),
            key_back.reshape(row_count, column_count),
            pair_grad[1],
        ],
        axis=1,
    ).astype(jnp.bfloat16)
    inner_grad = jnp.einsum("rc,dc->rd", qkv_low, full_qkv, preferred_element_type=jnp.float32)
    attended_flat = attended_low.reshape(row_count, column_count)
    share_width = feature_count // lax.axis_size("tensor")
    whole_sum = lax.psum(inner_grad.astype(jnp.bfloat16), "tensor").astype(jnp.float32)
    branch = lax.dynamic_slice_in_dim(
        normalize_back(whole_sum, normed, inverse),
        lax.axis_index("tensor") * share_width,
        share_width,
        1,
    )
    left_rows = unit_low
    right_rows = grad_rows
    qkv_term = jnp.einsum(
        "rd,rc->dc", left_rows, qkv_low, preferred_element_type=jnp.float32
    ).reshape(lax.axis_size(("seq", "dp")) * own_rows, 3, column_count)
    out_term = jnp.einsum(
        "rd,rc->dc", right_rows, attended_flat, preferred_element_type=jnp.float32
    )
    summed = lax.psum_scatter(
        jnp.concatenate([qkv_term, out_term[:, None, :]], axis=1).astype(jnp.bfloat16),
        ("seq", "dp"),
        scatter_dimension=0,
        tiled=True,
    ).astype(jnp.float32)
    return (summed[:, :3], summed[:, 3], branch.astype(jnp.bfloat16)[None])


def solution(mesh):
    return jax.shard_map(
        local,
        mesh=mesh,
        in_specs=(
            P("dp", "seq", None),
            P("dp", "seq", None),
            P(("seq", "dp"), None, "tensor"),
            P(("seq", "dp"), "tensor"),
        ),
        out_specs=(
            P(("seq", "dp"), None, "tensor"),
            P(("seq", "dp"), "tensor"),
            P("dp", "seq", "tensor"),
        ),
        check_vma=False,
    )
```

profile of v0, /device:TPU:0, one launch (start us, length us, event | category | flops | bytes accessed | tf_op | source)
XLA Modules:
  0.0 413.4 jit_solution(1419548005790425770)
XLA Ops:
  7.2 2.0 copy.55
  9.3 0.7 all-gather.8.cloned.1.call-update
  10.0 1.7 convert_reduce_fusion
  11.8 0.6 fusion.6
  12.3 67.3 %all-gather.4.cloned.1.call-done = bf16[3072,1152]{1,0:T(8,128)(2,1)} async-done(((bf16[192,1152]{1,0:T(8,128)(2,1)}), bf16[3072,1152]{1,0:T(8,128)(2,1)}) %all-gather.4.cloned.1.call-update) | async-done | bytes 7077904 | tf_op jit(solution)/shard_map/all_gather | solution.py:34
  79.6 5.3 %fusion.23 = f32[256,1152]{1,0:T(8,128)S(1)} fusion(bf16[3072,1152]{1,0:T(8,128)(2,1)} %all-gather.4.cloned.1.call-done, bf16[1,256,3072]{2,1,0:T(8,128)(2,1)S(1)} %copy-done.1, f32[256]{0:T(256)S(1)} %add_rsqrt_fusion.2, f32[256]{0:T(256)S(1)} %broadcast_multiply_fusion.8), kind=kOutput, calls=%fused_computation.35 | convolution fusion | flops 1815085056 | bytes 9832448 | tf_op jit(solution)/shard_map/dot_general | solution.py:39
  84.9 1.0 copy-done.7
  85.9 0.8 slice.45
  86.7 1.2 copy.27
  87.9 0.1 multiply_reduce_fusion.5
  88.0 0.8 mul.130
  88.8 1.9 copy.29
  90.7 0.8 sub.89
  91.5 1.9 copy.28
  93.5 1.0 fusion.49
  94.5 2.2 fusion.59
  96.7 0.8 pad_maximum_fusion.3
  97.5 25.5 %all-gather.8.cloned.1.call-done = bf16[3072,384]{1,0:T(8,128)(2,1)} async-done(((bf16[192,384]{1,0:T(8,128)(2,1)}), bf16[3072,384]{1,0:T(8,128)(2,1)}) %all-gather.8.cloned.1.call-update) | async-done | bytes 2359312 | tf_op jit(solution)/shard_map/all_gather | solution.py:35
  123.0 2.6 fusion.39
  125.7 0.8 copy.34
  126.5 1.2 copy.31
  127.7 0.1 multiply_reduce_fusion.4
  127.8 33.2 %all-gather.6.cloned.1.call-done = bf16[2,1024,384]{2,1,0:T(8,128)(2,1)} async-done(((bf16[2,256,384]{2,1,0:T(8,128)(2,1)}), bf16[2,1024,384]{2,1,0:T(8,128)(2,1)}) %all-gather.6.cloned.1.call-update) | async-done | bytes 1572880 | tf_op jit(solution)/shard_map/all_gather | solution.py:70
  161.0 2.7 fusion.58
  163.6 2.3 copy.30
  166.0 2.3 copy.35
  168.2 2.0 fusion.9
  170.3 1.7 fusion.27
  171.9 1.3 multiply_reduce_fusion.3
  173.3 1.1 multiply_convert_fusion
  174.4 1.2 copy-done.3
  175.6 1.3 convolution_convert_fusion.3
  176.9 2.3 copy.38
  179.2 2.3 copy.39
  181.5 2.7 pad_maximum_fusion.1
  184.2 0.2 all-reduce.2.cloned.1.call-start
  184.5 2.3 fusion.57
  186.8 0.8 multiply_convert_fusion.1
  187.6 1.7 copy.44
  189.3 29.4 %reduce-scatter.3.cloned.1.call-done = bf16[2,256,384]{2,1,0:T(8,128)(2,1)} async-done(((bf16[2,1024,384]{2,1,0:T(8,128)(2,1)}), bf16[2,256,384]{2,1,0:T(8,128)(2,1)}) %reduce-scatter.3.cloned.1.call-update) | async-done | bytes 393232 | tf_op jit(solution)/shard_map/reduce_scatter | solution.py:104
  218.7 1.9 slice_convert_fusion.1
  220.6 1.9 copy.40
  222.5 1.2 multiply_reduce_fusion.1
  223.7 0.8 mul.146
  224.5 1.9 copy.42
  226.4 0.8 sub.100
  227.2 1.9 copy.41
  229.1 1.6 fusion.46
  230.7 0.7 copy-done.8
  231.4 6.5 %convolution_convert_fusion.2 = bf16[256,3072]{1,0:T(8,128)(2,1)} fusion(bf16[3072,1152]{1,0:T(8,128)(2,1)} %all-gather.4.cloned.1.call-done, bf16[256,384]{1,0:T(8,128)(2,1)S(1)} %copy-done.13, bf16[256,384]{1,0:T(8,128)(2,1)S(1)} %fusion.46, bf16[256,384]{1,0:T(8,128)(2,1)S(1)} %copy-done.10), kind=kOutput, calls=%fused_computation.7 | convolution fusion | flops 1814495232 | bytes 9240576 | tf_op jit(solution)/shard_map/rc,dc->rd/dot_general | solution.py:117
  237.9 0.0 reduce-scatter.5.cloned.1.call-start
  238.0 3.5 fusion
  241.5 0.9 fusion.48
  242.4 2.2 copy.45
  244.5 5.5 %convolution_convert_fusion = bf16[3072,3,384]{2,0,1:T(8,128)(2,1)} fusion(bf16[3,384,256]{2,1,0:T(8,128)(2,1)} %bitcast.107, bf16[1,256,3072]{2,1,0:T(8,128)(2,1)S(1)} %copy-done.1, f32[256]{0:T(256)S(1)} %copy-done.17, f32[256]{0:T(256)S(1)} %copy-done.19), kind=kOutput, calls=%fused_computation.1 | convolution fusion | flops 1818624000 | bytes 9242624 | tf_op jit(solution)/shard_map/rd,rc->dc/dot_general | solution.py:129
  250.1 8.4 %pad_maximum_fusion = bf16[3072,4,384]{2,0,1:T(8,128)(2,1)} fusion(bf16[3072,1,384]{2,0,1:T(8,128)(2,1)} %fusion, bf16[3072,3,384]{2,0,1:T(8,128)(2,1)} %convolution_convert_fusion), kind=kLoop, calls=%fused_computation | loop fusion | flops 4718592 | bytes 18874368 | tf_op jit(solution)/shard_map/concatenate | solution.py:136
  258.5 29.9 %all-reduce.2.cloned.1.call-done = bf16[256,3072]{1,0:T(8,128)(2,1)} async-done(((bf16[256,3072]{1,0:T(8,128)(2,1)}), bf16[256,3072]{1,0:T(8,128)(2,1)}) %all-reduce.2.cloned.1.call-update) | async-done | bytes 1572880 | tf_op jit(solution)/shard_map/psum | solution.py:120
  288.4 1.9 convert_element_type.80
  290.3 1.1 convert_reduce_fusion.1
  291.4 1.2 fusion.43
  292.6 111.0 %reduce-scatter.5.cloned.1.call-done = bf16[192,4,384]{2,0,1:T(8,128)(2,1)} async-done(((bf16[3072,4,384]{2,0,1:T(8,128)(2,1)}), bf16[192,4,384]{2,0,1:T(8,128)(2,1)}) %reduce-scatter.5.cloned.1.call-update) | async-done | bytes 589840 | tf_op jit(solution)/shard_map/reduce_scatter | solution.py:135
  403.6 1.2 convert_element_type.78
  404.9 0.7 slice_bitcast_fusion
  405.6 1.0 slice.52
  (58 shorter events, 0.5 us)
Async XLA Ops:
  7.2 115.9 %copy-start = (bf16[1,256,3072]{2,1,0:T(8,128)(2,1)S(1)}, bf16[1,256,3072]{2,1,0:T(8,128)(2,1)}, u32[]{:S(2)}) copy-start(bf16[1,256,3072]{2,1,0:T(8,128)(2,1)} %param.5) | copy-start | bytes 4718596
  7.2 4.6 %copy-start.1 = (bf16[1,256,3072]{2,1,0:T(8,128)(2,1)S(1)}, bf16[1,256,3072]{2,1,0:T(8,128)(2,1)}, u32[]{:S(2)}) copy-start(bf16[1,256,3072]{2,1,0:T(8,128)(2,1)} %param.4) | copy-start | bytes 4718596
  7.2 72.5 %all-gather.4.cloned.1.call-start = ((), (), s32[]{:S(2)}) async-start(), calls=%async_computation.2 | async-start | bytes 7520256 | tf_op jit(solution)/shard_map/all_gather | solution.py:34
  9.2 113.8 %all-gather.8.cloned.1.call-start = ((), (), s32[]{:S(2)}) async-start(), calls=%async_computation.4 | async-start | bytes 2506752 | tf_op jit(solution)/shard_map/all_gather | solution.py:35
  10.0 151.0 %all-gather.6.cloned.1.call-start = ((), (), s32[]{:S(2)}) async-start(), calls=%async_computation.3 | async-start | bytes 1966080 | tf_op jit(solution)/shard_map/all_gather | solution.py:70
  11.7 73.2 %copy-start.18 = (f32[256]{0:T(256)}, f32[256]{0:T(256)S(1)}, u32[]{:S(2)}) copy-start(f32[256]{0:T(256)S(1)} %broadcast_multiply_fusion.8) | copy-start | bytes 3076
  12.3 72.6 %copy-start.16 = (f32[256]{0:T(256)}, f32[256]{0:T(256)S(1)}, u32[]{:S(2)}) copy-start(f32[256]{0:T(256)S(1)} %add_rsqrt_fusion.2) | copy-start | bytes 3076
  84.9 1.0 copy-start.7
  87.9 8.8 %copy-start.2 = (f32[256,384]{0,1:T(8,128)}, f32[256,384]{0,1:T(8,128)S(1)}, u32[]{:S(2)}) copy-start(f32[256,384]{0,1:T(8,128)S(1)} %copy.27) | copy-start | bytes 1179652
  97.5 121.2 %reduce-scatter.3.cloned.1.call-start = ((), (), s32[]{:S(2)}) async-start(), calls=%async_computation.5 | async-start | bytes 1966080 | tf_op jit(solution)/shard_map/reduce_scatter | solution.py:104
  168.2 2.0 copy-start.15
  170.2 1.7 copy-start.12
  174.4 1.2 copy-start.3
  184.2 104.2 %all-reduce.2.cloned.1.call-start = ((), (), s32[]{:S(2)}) async-start(), calls=%async_computation.7 | async-start | bytes 3145728 | tf_op jit(solution)/shard_map/psum | solution.py:120
  189.3 39.8 %copy-start.6 = (f32[256,384]{1,0:T(8,128)S(1)}, f32[256,384]{1,0:T(8,128)}, u32[]{:S(2)}) copy-start(f32[256,384]{1,0:T(8,128)} %copy.29) | copy-start | bytes 1179652
  229.1 2.3 copy-start.10
  229.1 2.3 copy-start.13
  230.7 0.7 copy-start.8
  237.9 3.6 copy-start.9
  237.9 3.6 copy-start.11
  237.9 165.7 %reduce-scatter.5.cloned.1.call-start = ((), (), s32[]{:S(2)}) async-start(), calls=%async_computation.6 | async-start | bytes 10027008 | tf_op jit(solution)/shard_map/reduce_scatter | solution.py:135
  238.0 3.6 copy-start.14
  238.0 6.6 %copy-start.17 = (f32[256]{0:T(256)S(1)}, f32[256]{0:T(256)}, u32[]{:S(2)}) copy-start(f32[256]{0:T(256)} %copy-done.16) | copy-start | bytes 3076
  238.0 6.6 %copy-start.19 = (f32[256]{0:T(256)S(1)}, f32[256]{0:T(256)}, u32[]{:S(2)}) copy-start(f32[256]{0:T(256)} %copy-done.18) | copy-start | bytes 3076
  288.4 1.9 copy-start.4
  403.6 2.0 copy-start.5
Sparse Core Ops, SparseCore 0:
  10.9 68.7 all-gather.3
  81.9 41.0 all-gather.7
  125.2 35.7 all-gather.5
  184.4 34.2 reduce-scatter.2
  238.0 50.3 all-reduce.1
  292.4 111.2 reduce-scatter.4
where the time goes:
time: 415 us; the launch traced here: 413 us
  waiting for transfers between devices  297 us (72%)
  local copies, waits for them, and re-layouts  40.1 us (10%)
  matrix products  33.2 us (8%)
  other arithmetic  28.3 us (7%)
  between operations  14.4 us (3%)
    reduce_scatter x1, waiting for transfers between devices, local(): lax.psum_scatter(jnp.concatenate([qkv_term, out_term[:, None, :]], axis=1...  111 us
    all_gather x1, waiting for transfers between devices, local(): piece_qkv = lax.all_gather(flat_weight, ('seq', 'dp'), axis=0, tiled=True)  67.3 us
    all_gather x1, waiting for transfers between devices, local(): every_pair = lax.all_gather(key_value, 'seq', axis=1, tiled=True)  33.2 us
    psum x1, waiting for transfers between devices, local(): lax.psum(inner_grad.astype(jnp.bfloat16), 'tensor').astype(jnp.float32)  29.9 us
    reduce_scatter x1, waiting for transfers between devices, local(): lax.psum_scatter(every_grad.astype(jnp.bfloat16), 'seq', scatter_dimensio...  29.4 us
    all_gather x1, waiting for transfers between devices, local(): piece_out = lax.all_gather(out_weight, ('seq', 'dp'), axis=0, tiled=True)  25.5 us
    concatenate x1, other arithmetic, local(): jnp.concatenate([qkv_term, out_term[:, None, :]], axis=1)  8.4 us
  transfers between devices with their start and end apart: 6, of which 6 were waited for; matrix products, arithmetic and copies ran while one was open for 13% of the time, Pallas kernels for 0%

commit v1 on v0

--- a/solution.py
+++ b/solution.py
@@ -67,7 +67,8 @@
             * score_scale
         )
 
-    every_pair = lax.all_gather(key_value, "seq", axis=1, tiled=True)
+    stack = jnp.stack([key_value] * lax.axis_size("seq"))
+    every_pair = jnp.concatenate(lax.all_to_all(stack, "seq", 0, 0), axis=1)
     piece_rows = every_pair.shape[1]
     exponent = jnp.exp(scores_of(every_pair[0]))
     add_exp_total = jnp.sum(exponent, axis=-1)

time: 415 us -> 408 us (0.983)
  waiting for transfers between devices: 297 us -> 280 us
  local copies, waits for them, and re-layouts: 40.1 us -> 47.4 us
  starting transfers between devices: 0.42 us -> 4.94 us
    all_gather x1 -> x0, waiting for transfers between devices: 33.2 us -> none  [local(): every_pair = lax.all_gather(key_value, 'seq', axis=1, tiled=True)]
    all_to_all x0 -> x1, waiting for transfers between devices: none -> 13.5 us  [local(): every_pair = jnp.concatenate(lax.all_to_all(stack, 'seq', 0, 0), axis=1)]
    another operation x0 -> x3, local copies, waits for them, and re-layouts: none -> 7.29 us  [the longest x1 2.54 us: local(): key_rows = every_pair[0].reshape(piece_rows, head_count, HD)]
    all_to_all x0 -> x1, starting transfers between devices: none -> 4.34 us  [local(): every_pair = jnp.concatenate(lax.all_to_all(stack, 'seq', 0, 0), axis=1)]
  transfers between devices with their start and end apart: 6 -> 6, of which waited for: 6 -> 6; matrix products, arithmetic and copies ran while one was open for 13% -> 14% of each run, Pallas kernels for 0% -> 0%
where the time goes in v1:
time: 408 us; the launch traced here: 407 us
  waiting for transfers between devices  280 us (69%)
  local copies, waits for them, and re-layouts  47.4 us (12%)
  matrix products  33.1 us (8%)
  other arithmetic  27.6 us (7%)
  between operations  14.1 us (3%)
  starting transfers between devices  4.94 us (1%)
    reduce_scatter x1, waiting for transfers between devices, local(): lax.psum_scatter(jnp.concatenate([qkv_term, out_term[:, None, :]], axis=1...  111 us
    all_gather x1, waiting for transfers between devices, local(): piece_qkv = lax.all_gather(flat_weight, ('seq', 'dp'), axis=0, tiled=True)  67.4 us
    psum x1, waiting for transfers between devices, local(): lax.psum(inner_grad.astype(jnp.bfloat16), 'tensor').astype(jnp.float32)  29.8 us
    reduce_scatter x1, waiting for transfers between devices, local(): lax.psum_scatter(every_grad.astype(jnp.bfloat16), 'seq', scatter_dimensio...  28.8 us
    all_gather x1, waiting for transfers between devices, local(): piece_out = lax.all_gather(out_weight, ('seq', 'dp'), axis=0, tiled=True)  28.7 us
    all_to_all x1, waiting for transfers between devices, local(): every_pair = jnp.concatenate(lax.all_to_all(stack, 'seq', 0, 0), axis=1)  13.5 us
    concatenate x1, other arithmetic, local(): jnp.concatenate([qkv_term, out_term[:, None, :]], axis=1)  8.4 us
  transfers between devices with their start and end apart: 6, of which 6 were waited for; matrix products, arithmetic and copies ran while one was open for 14% of the time, Pallas kernels for 0%

profile of v1, /device:TPU:0, one launch (start us, length us, event | category | flops | bytes accessed | tf_op | source)
XLA Modules:
  0.0 407.0 jit_solution(15388398001577949873)
XLA Ops:
  7.2 2.0 copy.75
  9.3 0.7 all-gather.5.cloned.1.call-update
  10.0 1.7 convert_reduce_fusion
  11.7 0.6 fusion.6
  12.3 67.4 %all-gather.3.cloned.1.call-done = bf16[3072,1152]{1,0:T(8,128)(2,1)} async-done(((bf16[192,1152]{1,0:T(8,128)(2,1)}), bf16[3072,1152]{1,0:T(8,128)(2,1)}) %all-gather.3.cloned.1.call-update) | async-done | bytes 7077904 | tf_op jit(solution)/shard_map/all_gather | solution.py:34
  79.6 5.3 %fusion.23 = f32[256,1152]{1,0:T(8,128)S(1)} fusion(bf16[3072,1152]{1,0:T(8,128)(2,1)} %all-gather.3.cloned.1.call-done, bf16[1,256,3072]{2,1,0:T(8,128)(2,1)S(1)} %copy-done.1, f32[256]{0:T(256)S(1)} %add_rsqrt_fusion.2, f32[256]{0:T(256)S(1)} %broadcast_multiply_fusion.8), kind=kOutput, calls=%fused_computation.35 | convolution fusion | flops 1815085056 | bytes 9832448 | tf_op jit(solution)/shard_map/dot_general | solution.py:39
  84.9 1.1 copy-done.7
  86.0 0.8 slice.47
  86.8 1.2 copy.46
  88.1 0.8 mul.130
  88.9 1.9 copy.48
  90.8 0.8 sub.89
  91.6 1.9 copy.47
  93.5 1.0 fusion.49
  94.5 2.2 fusion.59
  96.7 0.9 copy.49
  97.6 2.2 stack.19
  99.9 4.3 %all-to-all-start = ((bf16[4,2,256,384]{2,3,1,0:T(8,128)(2,1)}), bf16[4,2,256,384]{2,3,1,0:T(8,128)(2,1)}, u32[]{:S(2)}, u32[]{:S(2)}) async-start(bf16[4,2,256,384]{2,3,1,0:T(8,128)(2,1)} %stack.19), calls=%async_computation | async-start | bytes 3145728 | tf_op jit(solution)/shard_map/all_to_all | solution.py:71
  104.5 28.7 %all-gather.5.cloned.1.call-done = bf16[3072,384]{1,0:T(8,128)(2,1)} async-done(((bf16[192,384]{1,0:T(8,128)(2,1)}), bf16[3072,384]{1,0:T(8,128)(2,1)}) %all-gather.5.cloned.1.call-update) | async-done | bytes 2359312 | tf_op jit(solution)/shard_map/all_gather | solution.py:35
  133.2 2.6 fusion.39
  135.8 0.8 copy.54
  136.7 1.2 copy.51
  138.0 13.5 %all-to-all-done = bf16[4,2,256,384]{2,3,1,0:T(8,128)(2,1)} async-done(((bf16[4,2,256,384]{2,3,1,0:T(8,128)(2,1)}), bf16[4,2,256,384]{2,3,1,0:T(8,128)(2,1)}, u32[]{:S(2)}, u32[]{:S(2)}) %all-to-all-start) | async-done | bytes 1572896 | tf_op jit(solution)/shard_map/all_to_all | solution.py:71
  151.4 2.4 fusion.58
  153.8 1.5 copy.50
  155.3 2.5 reshape_squeeze.14
  157.8 2.6 copy.55
  160.4 2.5 reshape_squeeze.15
  162.9 2.0 fusion.9
  165.0 1.7 fusion.27
  166.6 1.3 multiply_reduce_fusion.3
  168.0 1.1 multiply_convert_fusion
  169.1 1.2 copy-done.3
  170.3 1.3 convolution_convert_fusion.3
  171.6 2.3 copy.58
  173.9 2.3 copy.59
  176.2 2.7 pad_maximum_fusion.1
  179.0 2.3 fusion.57
  181.3 0.8 multiply_convert_fusion.1
  182.1 1.8 copy.64
  183.9 28.8 %reduce-scatter.3.cloned.1.call-done = bf16[2,256,384]{2,1,0:T(8,128)(2,1)} async-done(((bf16[2,1024,384]{2,1,0:T(8,128)(2,1)}), bf16[2,256,384]{2,1,0:T(8,128)(2,1)}) %reduce-scatter.3.cloned.1.call-update) | async-done | bytes 393232 | tf_op jit(solution)/shard_map/reduce_scatter | solution.py:105
  212.7 1.9 slice_convert_fusion.1
  214.5 1.9 copy.60
  216.4 1.2 multiply_reduce_fusion.1
  217.7 0.8 mul.146
  218.4 1.9 copy.62
  220.3 0.8 sub.100
  221.1 1.9 copy.61
  223.0 1.6 fusion.46
  224.6 0.7 copy-done.8
  225.3 6.5 %convolution_convert_fusion.2 = bf16[256,3072]{1,0:T(8,128)(2,1)} fusion(bf16[3072,1152]{1,0:T(8,128)(2,1)} %all-gather.3.cloned.1.call-done, bf16[256,384]{1,0:T(8,128)(2,1)S(1)} %copy-done.13, bf16[256,384]{1,0:T(8,128)(2,1)S(1)} %fusion.46, bf16[256,384]{1,0:T(8,128)(2,1)S(1)} %copy-done.10), kind=kOutput, calls=%fused_computation.7 | convolution fusion | flops 1814495232 | bytes 9240576 | tf_op jit(solution)/shard_map/rc,dc->rd/dot_general | solution.py:118
  232.1 3.4 fusion
  235.6 0.9 fusion.48
  236.4 2.1 copy.65
  238.6 5.5 %convolution_convert_fusion = bf16[3072,3,384]{2,0,1:T(8,128)(2,1)} fusion(bf16[3,384,256]{2,1,0:T(8,128)(2,1)} %bitcast.108, bf16[1,256,3072]{2,1,0:T(8,128)(2,1)S(1)} %copy-done.1, f32[256]{0:T(256)S(1)} %copy-done.17, f32[256]{0:T(256)S(1)} %copy-done.19), kind=kOutput, calls=%fused_computation.1 | convolution fusion | flops 1818624000 | bytes 9242624 | tf_op jit(solution)/shard_map/rd,rc->dc/dot_general | solution.py:130
  244.1 8.4 %pad_maximum_fusion = bf16[3072,4,384]{2,0,1:T(8,128)(2,1)} fusion(bf16[3072,1,384]{2,0,1:T(8,128)(2,1)} %fusion, bf16[3072,3,384]{2,0,1:T(8,128)(2,1)} %convolution_convert_fusion), kind=kLoop, calls=%fused_computation | loop fusion | flops 4718592 | bytes 18874368 | tf_op jit(solution)/shard_map/concatenate | solution.py:137
  252.5 29.8 %all-reduce.2.cloned.1.call-done = bf16[256,3072]{1,0:T(8,128)(2,1)} async-done(((bf16[256,3072]{1,0:T(8,128)(2,1)}), bf16[256,3072]{1,0:T(8,128)(2,1)}) %all-reduce.2.cloned.1.call-update) | async-done | bytes 1572880 | tf_op jit(solution)/shard_map/psum | solution.py:121
  282.4 1.9 convert_element_type.80
  284.2 1.1 convert_reduce_fusion.1
  285.4 1.2 fusion.43
  286.6 111.0 %reduce-scatter.5.cloned.1.call-done = bf16[192,4,384]{2,0,1:T(8,128)(2,1)} async-done(((bf16[3072,4,384]{2,0,1:T(8,128)(2,1)}), bf16[192,4,384]{2,0,1:T(8,128)(2,1)}) %reduce-scatter.5.cloned.1.call-update) | async-done | bytes 589840 | tf_op jit(solution)/shard_map/reduce_scatter | solution.py:136
  397.6 1.2 convert_element_type.78
  398.8 0.7 slice_bitcast_fusion
  399.5 1.0 slice.54
  (61 shorter events, 1.1 us)
Async XLA Ops:
  7.2 126.0 %copy-start = (bf16[1,256,3072]{2,1,0:T(8,128)(2,1)S(1)}, bf16[1,256,3072]{2,1,0:T(8,128)(2,1)}, u32[]{:S(2)}) copy-start(bf16[1,256,3072]{2,1,0:T(8,128)(2,1)} %param.5) | copy-start | bytes 4718596
  7.2 4.5 %copy-start.1 = (bf16[1,256,3072]{2,1,0:T(8,128)(2,1)S(1)}, bf16[1,256,3072]{2,1,0:T(8,128)(2,1)}, u32[]{:S(2)}) copy-start(bf16[1,256,3072]{2,1,0:T(8,128)(2,1)} %param.4) | copy-start | bytes 4718596
  7.2 72.5 %all-gather.3.cloned.1.call-start = ((), (), s32[]{:S(2)}) async-start(), calls=%async_computation.3 | async-start | bytes 7520256 | tf_op jit(solution)/shard_map/all_gather | solution.py:34
  9.2 124.0 %all-gather.5.cloned.1.call-start = ((), (), s32[]{:S(2)}) async-start(), calls=%async_computation.4 | async-start | bytes 2506752 | tf_op jit(solution)/shard_map/all_gather | solution.py:35
  11.7 73.2 %copy-start.18 = (f32[256]{0:T(256)}, f32[256]{0:T(256)S(1)}, u32[]{:S(2)}) copy-start(f32[256]{0:T(256)S(1)} %broadcast_multiply_fusion.8) | copy-start | bytes 3076
  12.3 72.6 %copy-start.16 = (f32[256]{0:T(256)}, f32[256]{0:T(256)S(1)}, u32[]{:S(2)}) copy-start(f32[256]{0:T(256)S(1)} %add_rsqrt_fusion.2) | copy-start | bytes 3076
  84.9 1.1 copy-start.7
  88.0 8.7 %copy-start.2 = (f32[256,384]{0,1:T(8,128)}, f32[256,384]{0,1:T(8,128)S(1)}, u32[]{:S(2)}) copy-start(f32[256,384]{0,1:T(8,128)S(1)} %copy.46) | copy-start | bytes 1179652
  99.9 51.5 %all-to-all-start = ((bf16[4,2,256,384]{2,3,1,0:T(8,128)(2,1)}), bf16[4,2,256,384]{2,3,1,0:T(8,128)(2,1)}, u32[]{:S(2)}, u32[]{:S(2)}) async-start(bf16[4,2,256,384]{2,3,1,0:T(8,128)(2,1)} %stack.19), calls=%async_computation | async-start | bytes 3145728 | tf_op jit(solution)/shard_map/all_to_all | solution.py:71
  104.2 108.4 %reduce-scatter.3.cloned.1.call-start = ((), (), s32[]{:S(2)}) async-start(), calls=%async_computation.5 | async-start | bytes 1966080 | tf_op jit(solution)/shard_map/reduce_scatter | solution.py:105
  162.9 2.0 copy-start.15
  164.9 1.7 copy-start.12
  169.1 1.2 copy-start.3
  178.9 103.4 %all-reduce.2.cloned.1.call-start = ((), (), s32[]{:S(2)}) async-start(), calls=%async_computation.7 | async-start | bytes 3145728 | tf_op jit(solution)/shard_map/psum | solution.py:121
  183.9 39.2 %copy-start.6 = (f32[256,384]{1,0:T(8,128)S(1)}, f32[256,384]{1,0:T(8,128)}, u32[]{:S(2)}) copy-start(f32[256,384]{1,0:T(8,128)} %copy.48) | copy-start | bytes 1179652
  223.0 2.3 copy-start.10
  223.0 2.3 copy-start.13
  224.6 0.7 copy-start.8
  231.8 3.7 copy-start.9
  231.8 3.7 copy-start.11
  231.8 165.7 %reduce-scatter.5.cloned.1.call-start = ((), (), s32[]{:S(2)}) async-start(), calls=%async_computation.6 | async-start | bytes 10027008 | tf_op jit(solution)/shard_map/reduce_scatter | solution.py:136
  232.1 3.5 copy-start.14
  232.1 6.4 %copy-start.17 = (f32[256]{0:T(256)S(1)}, f32[256]{0:T(256)}, u32[]{:S(2)}) copy-start(f32[256]{0:T(256)} %copy-done.16) | copy-start | bytes 3076
  232.1 6.4 %copy-start.19 = (f32[256]{0:T(256)S(1)}, f32[256]{0:T(256)}, u32[]{:S(2)}) copy-start(f32[256]{0:T(256)} %copy-done.18) | copy-start | bytes 3076
  282.4 1.9 copy-start.4
  397.6 2.0 copy-start.5
Sparse Core Ops, SparseCore 0:
  10.9 68.7 all-gather.2
  81.9 51.2 all-gather.4
  179.1 33.5 reduce-scatter.2
  231.9 50.3 all-reduce.1
  286.3 111.2 reduce-scatter.4
